TPU v7x, 32 devices: a whole 2x2x4 slice. The times are simulated.
32 devices in a mesh: dom: 16 (over z, y, x), col: 2 (over core).
Axes of the slice: x: 2, y: 2, z: 4, core: 2. Of those that a mesh axis runs over, the one named last changes fastest.
Arguments:
- features: bfloat16 [16384, 256], P(('dom', 'col')), may hold values from -6 to 6
- weight: bfloat16 [256, 256], replicated, may hold values from -0.375 to 0.375
- cotangent: bfloat16 [16384, 256], P(('dom', 'col')), may hold values from -6 to 6
- tile_values: bfloat16 [1280, 128, 128], P(('dom', 'col')), may hold values from -0.15625 to 0.15625
- tile_rows: int32 [1280], P(('dom', 'col')), may hold values from 0 to 7
- tile_cols: int32 [1280], P(('dom', 'col')), may hold values from 0 to 19, as said below
- tile_count: int32 [32], P(('dom', 'col')), may hold values from 20 to 40, as said below
- send_blocks: int32 [32, 16], P(('dom', 'col')), may hold values from 0 to 3
Outputs:
- output_rows: bfloat16 [16384, 256], P(('dom', 'col'))
- feature_grad: bfloat16 [16384, 256], P(('dom', 'col'))
- weight_grad: float32 [256, 256], replicated
Inputs may be any that keep to these rules, and one draw needn't show every extreme that they name: `tile_cols`: A value v below 4 names the device's own row block v; a value 4 + s names the row block that the device of partition s with the same col index sends to this partition; no receive slot is named by two tiles of one device. Only the first tile_count slots of a device's tiles are live; some device has all 40 live.
All inputs are finite; a program needn't handle non-finite values.
Results may differ from a plain program's by a relative error of at most 0.0049.
Values may be sent and summed in bfloat16 or wider, within the bound.
A program may use at most 128 MiB of HBM per device.

v0:
```python
import jax
import jax.numpy as jnp
from jax import lax
from jax.sharding import PartitionSpec as P


def local(features, weight, cotangent, tile_values, tile_rows, tile_cols, tile_count, send_blocks):
    block_size = tile_values.shape[1]
    half_blocks = features.shape[0] // block_size
    width_in = features.shape[1]
    peer_count = send_blocks.shape[1]
    all_blocks = half_blocks * lax.axis_size("col")
    node_total = features.shape[0] * lax.axis_size("col") * lax.axis_size("dom")
    own_blocks = features.reshape(half_blocks, block_size, width_in)
    outgoing = own_blocks[send_blocks[0]]
    incoming = lax.all_to_all(outgoing, "dom", split_axis=0, concat_axis=0, tiled=True)
    sources = jnp.concatenate([own_blocks, incoming], axis=0)
    live_bool = jnp.arange(tile_values.shape[0], dtype=jnp.int32) < tile_count[0]
    live_mask = live_bool.astype(jnp.bfloat16)
    masked_tiles = tile_values * live_mask[:, None, None]
    picked = sources[tile_cols]
    products = jnp.einsum("tij,tjf->tif", masked_tiles, picked, preferred_element_type=jnp.float32)
    partial_value = jax.ops.segment_sum(products, tile_rows, num_segments=all_blocks)
    summed = lax.psum_scatter(partial_value, "col", scatter_dimension=0, tiled=True)
    hidden = summed.astype(jnp.bfloat16).reshape(half_blocks * block_size, width_in)
    output_rows = jnp.dot(hidden, weight, preferred_element_type=jnp.float32).astype(jnp.bfloat16)
    own_grad = lax.dot_general(
        cotangent, weight, (((1,), (1,)), ((), ())), preferred_element_type=jnp.float32
    ).astype(jnp.bfloat16)
    own_grad = own_grad.reshape(half_blocks, block_size, width_in)
    grad_blocks = lax.all_gather(own_grad, "col", axis=0, tiled=True)
    chosen = grad_blocks[tile_rows]
    back_terms = jnp.einsum(
        "tji,tjf->tif", masked_tiles, chosen, preferred_element_type=jnp.float32
    )
    spread = jax.ops.segment_sum(back_terms, tile_cols, num_segments=half_blocks + peer_count)
    returned = lax.all_to_all(spread[half_blocks:], "dom", split_axis=0, concat_axis=0, tiled=True)
    grad_total = spread[:half_blocks] + jax.ops.segment_sum(
        returned, send_blocks[0], num_segments=half_blocks
    )
    feature_grad = grad_total.astype(jnp.bfloat16).reshape(half_blocks * block_size, width_in)
    local_weight = lax.dot_general(
        hidden, cotangent, (((0,), (0,)), ((), ())), preferred_element_type=jnp.float32
    )
    local_weight = local_weight * jnp.float32(1.0 / node_total**0.5)
    col_share = lax.psum_scatter(local_weight, "col", scatter_dimension=0, tiled=True)
    dom_share = lax.psum(col_share, "dom")
    weight_grad = lax.all_gather(dom_share, "col", axis=0, tiled=True)
    return (output_rows, feature_grad, weight_grad)


def solution(mesh):
    return jax.shard_map(
        local,
        mesh=mesh,
        in_specs=(
            P(("dom", "col"), None),
            P(),
            P(("dom", "col"), None),
            P(("dom", "col"), None, None),
            P(("dom", "col")),
            P(("dom", "col")),
            P(("dom", "col")),
            P(("dom", "col"), None),
        ),
        out_specs=(P(("dom", "col"), None), P(("dom", "col"), None), P()),
        check_vma=False,
    )
```

profile of v0, /device:TPU:0, one launch (start us, length us, event | category | flops | bytes accessed | tf_op | source)
XLA Modules:
  0.0 214.5 jit_solution(6143368337666922137)
XLA Ops:
  7.2 0.7 fusion.6
  7.9 2.6 %gather_fusion = bf16[16,128,256]{2,1,0:T(8,128)(2,1)} fusion(bf16[4,128,256]{2,1,0:T(8,128)(2,1)} %bitcast.19, s32[1024]{0:T(1024)S(1)} %pad_clamp_fusion.2), kind=kCustom, calls=%fused_computation | custom fusion | bytes 2097216 | tf_op jit(solution)/shard_map/gather | solution.py:15
  10.5 8.4 %all-to-all-start = ((bf16[16,128,256]{2,1,0:T(8,128)(2,1)}), bf16[16,128,256]{2,1,0:T(8,128)(2,1)}, u32[]{:S(2)}, u32[]{:S(2)}) async-start(bf16[16,128,256]{2,1,0:T(8,128)(2,1)} %gather_fusion), calls=%async_computation | async-start | bytes 2097152 | tf_op jit(solution)/shard_map/all_to_all | solution.py:16
  19.6 0.3 convolution_convert_fusion
  19.9 2.2 %all_gather.6 = bf16[8,128,256]{2,1,0:T(8,128)(2,1)S(1)} all-gather(bf16[4,128,256]{2,1,0:T(8,128)(2,1)S(1)} %bitcast.23), channel_id=1, replica_groups=mesh['dom'=16,'col'=2] {'col'}, dimensions={0}, use_global_device_ids=true | all-gather | bytes 786432 | tf_op jit(solution)/shard_map/all_gather | solution.py:31
  22.0 0.7 gather_fusion.2
  22.8 4.9 %fusion = f32[40,128,256]{2,1,0:T(8,128)} fusion(bf16[40,128,256]{2,1,0:T(8,128)(2,1)S(1)} %gather_fusion.2, bf16[40,128,128]{2,1,0:T(8,128)(2,1)} %param.11, bf16[40]{0:T(256)(128)(2,1)S(1)} %compare_convert_fusion), kind=kOutput, calls=%fused_computation.10 | convolution fusion | flops 336199680 | bytes 9175120 | tf_op jit(solution)/shard_map/tji,tjf->tif/dot_general | solution.py:33
  27.7 0.3 broadcast_in_dim.24
  28.0 0.4 copy-done.6
  28.4 9.1 %scatter_fusion.1 = f32[20,128,256]{2,1,0:T(8,128)S(1)} fusion(f32[20,128,256]{2,1,0:T(8,128)S(1)} %broadcast_in_dim.24, s32[40]{0:T(128)S(1)} %copy-done.6, f32[40,128,256]{2,1,0:T(8,128)} %fusion), kind=kCustom, calls=%fused_computation.4 | custom fusion | flops 1310720 | bytes 15728800 | tf_op jit(solution)/shard_map/scatter-add | solution.py:36
  37.4 1.8 slice.15
  39.2 4.1 %all-to-all-done = bf16[16,128,256]{2,1,0:T(8,128)(2,1)} async-done(((bf16[16,128,256]{2,1,0:T(8,128)(2,1)}), bf16[16,128,256]{2,1,0:T(8,128)(2,1)}, u32[]{:S(2)}, u32[]{:S(2)}) %all-to-all-start) | async-done | bytes 1048608 | tf_op jit(solution)/shard_map/all_to_all | solution.py:16
  43.3 5.9 %all-to-all-start.1 = ((f32[16,128,256]{2,1,0:T(8,128)}), f32[16,128,256]{2,1,0:T(8,128)}, u32[]{:S(2)}, u32[]{:S(2)}) async-start(f32[16,128,256]{2,1,0:T(8,128)} %slice.15), calls=%async_computation.2 | async-start | bytes 4194304 | tf_op jit(solution)/shard_map/all_to_all | solution.py:37
  49.4 1.3 pad_maximum_fusion
  50.7 2.4 %gather_fusion.1 = bf16[40,128,256]{2,1,0:T(8,128)(2,1)} fusion(bf16[20,128,256]{2,1,0:T(8,128)(2,1)S(1)} %pad_maximum_fusion, s32[1024]{0:T(1024)S(1)} %pad_clamp_fusion.1), kind=kCustom, calls=%fused_computation.1 | custom fusion | bytes 5243040 | tf_op jit(solution)/shard_map/gather | solution.py:21
  53.1 4.9 %fusion.2 = f32[40,128,256]{2,1,0:T(8,128)} fusion(bf16[40,128,256]{2,1,0:T(8,128)(2,1)} %gather_fusion.1, bf16[40,128,128]{2,1,0:T(8,128)(2,1)S(1)} %copy-done.4, bf16[40]{0:T(256)(128)(2,1)S(1)} %compare_convert_fusion), kind=kOutput, calls=%fused_computation.12 | convolution fusion | flops 336199680 | bytes 9175120 | tf_op jit(solution)/shard_map/tij,tjf->tif/dot_general | solution.py:22
  58.1 0.1 broadcast_in_dim.21
  58.1 9.0 %scatter_fusion = f32[8,128,256]{2,1,0:T(8,128)S(1)} fusion(f32[8,128,256]{2,1,0:T(8,128)S(1)} %broadcast_in_dim.21, s32[40]{0:T(128)S(1)} %copy-done.7, f32[40,128,256]{2,1,0:T(8,128)} %fusion.2), kind=kCustom, calls=%fused_computation.3 | custom fusion | flops 1310720 | bytes 15728800 | tf_op jit(solution)/shard_map/scatter-add | solution.py:23
  67.2 1.1 copy-done.1
  68.3 0.0 reduce-scatter.5.cloned.1.call-start
  68.4 9.7 %reduce-scatter.3.cloned.1.call-done = f32[4,128,256]{2,1,0:T(8,128)} async-done(((f32[8,128,256]{2,1,0:T(8,128)}), f32[4,128,256]{2,1,0:T(8,128)}) %reduce-scatter.3.cloned.1.call-update) | async-done | bytes 524304 | tf_op jit(solution)/shard_map/reduce_scatter | solution.py:24
  78.1 1.1 convert_element_type.20
  79.1 1.0 convolution_multiply_fusion
  80.1 0.0 all-reduce.2.cloned.1.call-start
  80.2 1.1 slice.14
  81.3 10.0 %all-to-all-done.1 = f32[16,128,256]{2,1,0:T(8,128)} async-done(((f32[16,128,256]{2,1,0:T(8,128)}), f32[16,128,256]{2,1,0:T(8,128)}, u32[]{:S(2)}, u32[]{:S(2)}) %all-to-all-start.1) | async-done | bytes 2097184 | tf_op jit(solution)/shard_map/all_to_all | solution.py:37
  91.2 3.5 %scatter_fusion.2 = f32[4,128,256]{2,1,0:T(8,128)S(1)} fusion(f32[4,128,256]{2,1,0:T(8,128)S(1)} %slice.14, s32[16]{0:T(128)S(1)} %bitcast.25, f32[16,128,256]{2,1,0:T(8,128)} %all-to-all-done.1), kind=kCustom, calls=%fused_computation.5 | custom fusion | flops 524288 | bytes 6291520 | tf_op jit(solution)/shard_map/scatter-add | solution.py:38
  94.7 0.7 convert_element_type.23
  95.5 0.9 convolution_convert_fusion.1
  96.4 108.7 %all-reduce.2.cloned.1.call-done = f32[128,256]{1,0:T(8,128)} async-done(((f32[128,256]{1,0:T(8,128)}), f32[128,256]{1,0:T(8,128)}) %all-reduce.2.cloned.1.call-update) | async-done | bytes 131088 | tf_op jit(solution)/shard_map/psum | solution.py:47
  205.1 2.2 %all_gather.7 = f32[256,256]{1,0:T(8,128)S(1)} all-gather(f32[128,256]{1,0:T(8,128)} %all-reduce.2.cloned.1.call-done), channel_id=1, replica_groups=mesh['dom'=16,'col'=2] {'col'}, dimensions={0}, use_global_device_ids=true | all-gather | bytes 393216 | tf_op jit(solution)/shard_map/all_gather | solution.py:48
  207.3 0.7 copy.20
  (27 shorter events, 0.2 us)
Async XLA Ops:
  7.2 12.4 %copy-start = (bf16[512,256]{1,0:T(8,128)(2,1)S(1)}, bf16[512,256]{1,0:T(8,128)(2,1)}, u32[]{:S(2)}) copy-start(bf16[512,256]{1,0:T(8,128)(2,1)} %param.10) | copy-start | bytes 786436
  7.2 12.4 %copy-start.7 = (s32[40]{0:T(128)S(1)}, s32[40]{0:T(128)}, u32[]{:S(2)}) copy-start(s32[40]{0:T(128)} %param.12) | copy-start | bytes 484
  7.2 12.4 %copy-start.5 = (bf16[256,256]{1,0:T(8,128)(2,1)S(1)}, bf16[256,256]{1,0:T(8,128)(2,1)}, u32[]{:S(2)}) copy-start(bf16[256,256]{1,0:T(8,128)(2,1)} %param.9) | copy-start | bytes 393220
  10.5 32.8 %all-to-all-start = ((bf16[16,128,256]{2,1,0:T(8,128)(2,1)}), bf16[16,128,256]{2,1,0:T(8,128)(2,1)}, u32[]{:S(2)}, u32[]{:S(2)}) async-start(bf16[16,128,256]{2,1,0:T(8,128)(2,1)} %gather_fusion), calls=%async_computation | async-start | bytes 2097152 | tf_op jit(solution)/shard_map/all_to_all | solution.py:16
  27.7 0.7 copy-start.6
  37.4 5.9 %copy-start.2 = (f32[20,128,256]{2,1,0:T(8,128)}, f32[20,128,256]{2,1,0:T(8,128)S(1)}, u32[]{:S(2)}) copy-start(f32[20,128,256]{2,1,0:T(8,128)S(1)} %scatter_fusion.1) | copy-start | bytes 7864324
  39.2 10.1 %copy-start.3 = (bf16[512,256]{1,0:T(8,128)(2,1)S(1)}, bf16[512,256]{1,0:T(8,128)(2,1)}, u32[]{:S(2)}) copy-start(bf16[512,256]{1,0:T(8,128)(2,1)} %param.8) | copy-start | bytes 786436
  43.3 47.9 %all-to-all-start.1 = ((f32[16,128,256]{2,1,0:T(8,128)}), f32[16,128,256]{2,1,0:T(8,128)}, u32[]{:S(2)}, u32[]{:S(2)}) async-start(f32[16,128,256]{2,1,0:T(8,128)} %slice.15), calls=%async_computation.2 | async-start | bytes 4194304 | tf_op jit(solution)/shard_map/all_to_all | solution.py:37
  49.3 28.8 %reduce-scatter.3.cloned.1.call-start = ((), (), s32[]{:S(2)}) async-start(), calls=%async_computation.4 | async-start | bytes 1572864 | tf_op jit(solution)/shard_map/reduce_scatter | solution.py:24
  50.7 2.4 %copy-start.4 = (bf16[40,128,128]{2,1,0:T(8,128)(2,1)S(1)}, bf16[40,128,128]{2,1,0:T(8,128)(2,1)}, u32[]{:S(2)}) copy-start(bf16[40,128,128]{2,1,0:T(8,128)(2,1)} %param.11) | copy-start | bytes 3932164
  67.2 1.1 copy-start.1
  67.2 24.0 %copy-start.8 = (s32[1,16]{1,0:T(1,128)S(1)}, s32[1,16]{1,0:T(1,128)}, u32[]{:S(2)}) copy-start(s32[1,16]{1,0:T(1,128)} %param.15) | copy-start | bytes 196
  68.3 27.1 %reduce-scatter.5.cloned.1.call-start = ((), (), s32[]{:S(2)}) async-start(), calls=%async_computation.5 | async-start | bytes 393216 | tf_op jit(solution)/shard_map/reduce_scatter | solution.py:46
  80.1 125.0 %all-reduce.2.cloned.1.call-start = ((), (), s32[]{:S(2)}) async-start(), calls=%async_computation.6 | async-start | bytes 262144 | tf_op jit(solution)/shard_map/psum | solution.py:47
Sparse Core Ops, SparseCore 0:
  68.4 9.5 reduce-scatter.2
  80.9 8.9 reduce-scatter.4
  95.6 109.4 all-reduce.1
where the time goes:
time: 215 us
  waiting for transfers between devices  133 us (62%)
  other arithmetic  25.5 us (12%)
  between operations  14.6 us (7%)
  starting transfers between devices  14.4 us (7%)
  matrix products  12 us (6%)
  local copies, waits for them, and re-layouts  11.1 us (5%)
  blocking collectives  4.37 us (2%)
    psum x1, waiting for transfers between devices, local(): dom_share = lax.psum(col_share, 'dom')  109 us
    all_to_all x1, waiting for transfers between devices, local(): lax.all_to_all(spread[half_blocks:], 'dom', split_axis=0, concat_axis=0,...  9.95 us
    reduce_scatter x1, waiting for transfers between devices, local(): lax.psum_scatter(partial_value, 'col', scatter_dimension=0, tiled=True)  9.71 us
    scatter-add x1, other arithmetic, local(): jax.ops.segment_sum(back_terms, tile_cols, num_segments=half_blocks + pee...  9.08 us
    scatter-add x1, other arithmetic, local(): jax.ops.segment_sum(products, tile_rows, num_segments=all_blocks)  9.04 us
    all_to_all x1, starting transfers between devices, local(): lax.all_to_all(outgoing, 'dom', split_axis=0, concat_axis=0, tiled=True)  8.39 us
    all_to_all x1, starting transfers between devices, local(): lax.all_to_all(spread[half_blocks:], 'dom', split_axis=0, concat_axis=0,...  5.93 us
    dot_general x1, matrix products, local(): jnp.einsum('tij,tjf->tif', masked_tiles, picked, preferred_element_type=j...  4.93 us
  transfers between devices with their start and end apart: 5, of which 4 were waited for; matrix products, arithmetic and copies ran while one was open for 20% of the time, Pallas kernels for 0%

commit v1 on v0

--- a/solution.py
+++ b/solution.py
@@ -44,7 +44,7 @@
     )
     local_weight = local_weight * jnp.float32(1.0 / node_total**0.5)
     col_share = lax.psum_scatter(local_weight, "col", scatter_dimension=0, tiled=True)
-    dom_share = lax.psum(col_share, "dom")
+    dom_share = jnp.sum(lax.all_gather(col_share, "dom"), axis=0)
     weight_grad = lax.all_gather(dom_share, "col", axis=0, tiled=True)
     return (output_rows, feature_grad, weight_grad)
 

time: 215 us -> 185 us (0.86)
  waiting for transfers between devices: 133 us -> 102 us
    psum x1 -> x0, waiting for transfers between devices: 109 us -> none  [local(): dom_share = lax.psum(col_share, 'dom')]
    all_to_all x1, waiting for transfers between devices: 9.95 us -> 48.3 us  [local(): lax.all_to_all(spread[half_blocks:], 'dom', split_axis=0, concat_axis=0,...]
    all_gather x0 -> x1, waiting for transfers between devices: none -> 24.1 us  [local(): dom_share = jnp.sum(lax.all_gather(col_share, 'dom'), axis=0)]
    all_to_all x1, waiting for transfers between devices: 4.13 us -> 23.6 us  [local(): lax.all_to_all(outgoing, 'dom', split_axis=0, concat_axis=0, tiled=True)]
    reduce_scatter x1, waiting for transfers between devices: 9.71 us -> 5.54 us  [local(): lax.psum_scatter(partial_value, 'col', scatter_dimension=0, tiled=True)]
  transfers between devices with their start and end apart: 5 -> 5, of which waited for: 4 -> 4; matrix products, arithmetic and copies ran while one was open for 20% -> 12% of each run, Pallas kernels for 0% -> 0%
where the time goes in v1:
time: 185 us
  waiting for transfers between devices  102 us (55%)
  other arithmetic  26 us (14%)
  starting transfers between devices  15.5 us (8%)
  between operations  14.6 us (8%)
  matrix products  12 us (6%)
  local copies, waits for them, and re-layouts  9.94 us (5%)
  blocking collectives  4.18 us (2%)
    all_to_all x1, waiting for transfers between devices, local(): lax.all_to_all(spread[half_blocks:], 'dom', split_axis=0, concat_axis=0,...  48.3 us
    all_gather x1, waiting for transfers between devices, local(): dom_share = jnp.sum(lax.all_gather(col_share, 'dom'), axis=0)  24.1 us
    all_to_all x1, waiting for transfers between devices, local(): lax.all_to_all(outgoing, 'dom', split_axis=0, concat_axis=0, tiled=True)  23.6 us
    scatter-add x1, other arithmetic, local(): jax.ops.segment_sum(back_terms, tile_cols, num_segments=half_blocks + pee...  9.1 us
    scatter-add x1, other arithmetic, local(): jax.ops.segment_sum(products, tile_rows, num_segments=all_blocks)  9.04 us
    all_to_all x1, starting transfers between devices, local(): lax.all_to_all(outgoing, 'dom', split_axis=0, concat_axis=0, tiled=True)  8.34 us
    all_to_all x1, starting transfers between devices, local(): lax.all_to_all(spread[half_blocks:], 'dom', split_axis=0, concat_axis=0,...  7.02 us
    reduce_scatter x1, waiting for transfers between devices, local(): lax.psum_scatter(partial_value, 'col', scatter_dimension=0, tiled=True)  5.54 us
  transfers between devices with their start and end apart: 5, of which 4 were waited for; matrix products, arithmetic and copies ran while one was open for 12% of the time, Pallas kernels for 0%

profile of v1, /device:TPU:0, one launch (start us, length us, event | category | flops | bytes accessed | tf_op | source)
XLA Modules:
  0.0 184.6 jit_solution(2431246527061912870)
XLA Ops:
  7.2 0.7 fusion.6
  7.9 2.5 %gather_fusion = bf16[16,128,256]{2,1,0:T(8,128)(2,1)} fusion(bf16[4,128,256]{2,1,0:T(8,128)(2,1)} %bitcast.20, s32[1024]{0:T(1024)S(1)} %pad_clamp_fusion.2), kind=kCustom, calls=%fused_computation | custom fusion | bytes 2097216 | tf_op jit(solution)/shard_map/gather | solution.py:15
  10.5 8.3 %all-to-all-start = ((bf16[16,128,256]{2,1,0:T(8,128)(2,1)}), bf16[16,128,256]{2,1,0:T(8,128)(2,1)S(1)}, u32[]{:S(2)}, u32[]{:S(2)}) async-start(bf16[16,128,256]{2,1,0:T(8,128)(2,1)} %gather_fusion), calls=%async_computation | async-start | bytes 2097152 | tf_op jit(solution)/shard_map/all_to_all | solution.py:16
  19.6 23.6 %all-to-all-done = bf16[16,128,256]{2,1,0:T(8,128)(2,1)S(1)} async-done(((bf16[16,128,256]{2,1,0:T(8,128)(2,1)}), bf16[16,128,256]{2,1,0:T(8,128)(2,1)S(1)}, u32[]{:S(2)}, u32[]{:S(2)}) %all-to-all-start) | async-done | bytes 1048608 | tf_op jit(solution)/shard_map/all_to_all | solution.py:16
  43.2 0.1 pad_maximum_fusion
  43.3 2.4 %gather_fusion.1 = bf16[40,128,256]{2,1,0:T(8,128)(2,1)} fusion(bf16[20,128,256]{2,1,0:T(8,128)(2,1)S(1)} %pad_maximum_fusion, s32[1024]{0:T(1024)S(1)} %pad_clamp_fusion.1), kind=kCustom, calls=%fused_computation.1 | custom fusion | bytes 5243040 | tf_op jit(solution)/shard_map/gather | solution.py:21
  45.7 4.9 %fusion.2 = f32[40,128,256]{2,1,0:T(8,128)} fusion(bf16[40,128,256]{2,1,0:T(8,128)(2,1)} %gather_fusion.1, bf16[40,128,128]{2,1,0:T(8,128)(2,1)S(1)} %copy-done.3, bf16[40]{0:T(256)(128)(2,1)S(1)} %compare_convert_fusion), kind=kOutput, calls=%fused_computation.12 | convolution fusion | flops 336199680 | bytes 9175120 | tf_op jit(solution)/shard_map/tij,tjf->tif/dot_general | solution.py:22
  50.6 0.1 broadcast_in_dim.21
  50.8 9.0 %scatter_fusion = f32[8,128,256]{2,1,0:T(8,128)S(1)} fusion(f32[8,128,256]{2,1,0:T(8,128)S(1)} %broadcast_in_dim.21, s32[40]{0:T(128)S(1)} %copy-done.7, f32[40,128,256]{2,1,0:T(8,128)} %fusion.2), kind=kCustom, calls=%fused_computation.3 | custom fusion | flops 1310720 | bytes 15728800 | tf_op jit(solution)/shard_map/scatter-add | solution.py:23
  59.8 1.0 copy-done.1
  60.9 0.3 convolution_convert_fusion
  61.2 2.2 %all_gather.12 = bf16[8,128,256]{2,1,0:T(8,128)(2,1)S(1)} all-gather(bf16[4,128,256]{2,1,0:T(8,128)(2,1)S(1)} %bitcast.25), channel_id=1, replica_groups=mesh['dom'=16,'col'=2] {'col'}, dimensions={0}, use_global_device_ids=true | all-gather | bytes 786432 | tf_op jit(solution)/shard_map/all_gather | solution.py:31
  63.3 0.7 gather_fusion.2
  64.1 5.5 %reduce-scatter.3.cloned.1.call-done = f32[4,128,256]{2,1,0:T(8,128)} async-done(((f32[8,128,256]{2,1,0:T(8,128)}), f32[4,128,256]{2,1,0:T(8,128)}) %reduce-scatter.3.cloned.1.call-update) | async-done | bytes 524304 | tf_op jit(solution)/shard_map/reduce_scatter | solution.py:24
  69.6 1.1 convert_element_type.20
  70.7 0.7 copy-done.4
  71.4 1.0 convolution_multiply_fusion
  72.4 4.9 %fusion = f32[40,128,256]{2,1,0:T(8,128)} fusion(bf16[40,128,256]{2,1,0:T(8,128)(2,1)S(1)} %gather_fusion.2, bf16[40,128,128]{2,1,0:T(8,128)(2,1)} %param.11, bf16[40]{0:T(256)(128)(2,1)S(1)} %compare_convert_fusion), kind=kOutput, calls=%fused_computation.10 | convolution fusion | flops 336199680 | bytes 9175120 | tf_op jit(solution)/shard_map/tji,tjf->tif/dot_general | solution.py:33
  77.3 0.3 broadcast_in_dim.24
  77.6 9.1 %scatter_fusion.1 = f32[20,128,256]{2,1,0:T(8,128)S(1)} fusion(f32[20,128,256]{2,1,0:T(8,128)S(1)} %broadcast_in_dim.24, s32[40]{0:T(128)S(1)} %copy-done.8, f32[40,128,256]{2,1,0:T(8,128)} %fusion), kind=kCustom, calls=%fused_computation.4 | custom fusion | flops 1310720 | bytes 15728800 | tf_op jit(solution)/shard_map/scatter-add | solution.py:36
  86.7 1.5 slice.15
  88.2 7.0 %all-to-all-start.1 = ((f32[16,128,256]{2,1,0:T(8,128)}), f32[16,128,256]{2,1,0:T(8,128)}, u32[]{:S(2)}, u32[]{:S(2)}) async-start(f32[16,128,256]{2,1,0:T(8,128)} %slice.15), calls=%async_computation.2 | async-start | bytes 4194304 | tf_op jit(solution)/shard_map/all_to_all | solution.py:37
  95.3 0.0 all-gather.3.cloned.1.call-start
  95.3 0.7 all-gather.3.cloned.1.call-update
  96.0 48.3 %all-to-all-done.1 = f32[16,128,256]{2,1,0:T(8,128)} async-done(((f32[16,128,256]{2,1,0:T(8,128)}), f32[16,128,256]{2,1,0:T(8,128)}, u32[]{:S(2)}, u32[]{:S(2)}) %all-to-all-start.1) | async-done | bytes 2097184 | tf_op jit(solution)/shard_map/all_to_all | solution.py:37
  144.3 3.5 %scatter_fusion.2 = f32[4,128,256]{2,1,0:T(8,128)S(1)} fusion(f32[4,128,256]{2,1,0:T(8,128)S(1)} %slice.14, s32[16]{0:T(128)S(1)} %bitcast.27, f32[16,128,256]{2,1,0:T(8,128)} %all-to-all-done.1), kind=kCustom, calls=%fused_computation.5 | custom fusion | flops 524288 | bytes 6291520 | tf_op jit(solution)/shard_map/scatter-add | solution.py:38
  147.8 0.7 convert_element_type.23
  148.6 0.9 convolution_convert_fusion.1
  149.5 24.1 %all-gather.3.cloned.1.call-done = f32[2048,256]{1,0:T(8,128)} async-done(((f32[128,256]{1,0:T(8,128)}), f32[2048,256]{1,0:T(8,128)}) %all-gather.3.cloned.1.call-update) | async-done | bytes 2097168 | tf_op jit(solution)/shard_map/all_gather | solution.py:47
  173.6 1.7 reduce_sum.9
  175.3 2.0 %all_gather.15 = f32[256,256]{1,0:T(8,128)S(1)} all-gather(f32[128,256]{1,0:T(8,128)S(1)} %reduce_sum.9), channel_id=1, replica_groups=mesh['dom'=16,'col'=2] {'col'}, dimensions={0}, use_global_device_ids=true | all-gather | bytes 393216 | tf_op jit(solution)/shard_map/all_gather | solution.py:48
  177.3 0.7 copy.19
  (30 shorter events, 0.3 us)
Async XLA Ops:
  7.2 53.7 %copy-start = (bf16[512,256]{1,0:T(8,128)(2,1)S(1)}, bf16[512,256]{1,0:T(8,128)(2,1)}, u32[]{:S(2)}) copy-start(bf16[512,256]{1,0:T(8,128)(2,1)} %param.10) | copy-start | bytes 786436
  7.2 36.0 %copy-start.2 = (bf16[512,256]{1,0:T(8,128)(2,1)S(1)}, bf16[512,256]{1,0:T(8,128)(2,1)}, u32[]{:S(2)}) copy-start(bf16[512,256]{1,0:T(8,128)(2,1)} %param.8) | copy-start | bytes 786436
  7.2 12.3 %copy-start.8 = (s32[40]{0:T(128)S(1)}, s32[40]{0:T(128)}, u32[]{:S(2)}) copy-start(s32[40]{0:T(128)} %param.13) | copy-start | bytes 484
  10.5 32.7 %all-to-all-start = ((bf16[16,128,256]{2,1,0:T(8,128)(2,1)}), bf16[16,128,256]{2,1,0:T(8,128)(2,1)S(1)}, u32[]{:S(2)}, u32[]{:S(2)}) async-start(bf16[16,128,256]{2,1,0:T(8,128)(2,1)} %gather_fusion), calls=%async_computation | async-start | bytes 2097152 | tf_op jit(solution)/shard_map/all_to_all | solution.py:16
  18.8 50.8 %reduce-scatter.3.cloned.1.call-start = ((), (), s32[]{:S(2)}) async-start(), calls=%async_computation.4 | async-start | bytes 1572864 | tf_op jit(solution)/shard_map/reduce_scatter | solution.py:24
  43.3 2.4 %copy-start.3 = (bf16[40,128,128]{2,1,0:T(8,128)(2,1)S(1)}, bf16[40,128,128]{2,1,0:T(8,128)(2,1)}, u32[]{:S(2)}) copy-start(bf16[40,128,128]{2,1,0:T(8,128)(2,1)} %param.11) | copy-start | bytes 3932164
  45.7 5.0 %copy-start.7 = (s32[40]{0:T(128)S(1)}, s32[40]{0:T(128)}, u32[]{:S(2)}) copy-start(s32[40]{0:T(128)} %param.12) | copy-start | bytes 484
  50.7 10.1 %copy-start.6 = (bf16[256,256]{1,0:T(8,128)(2,1)S(1)}, bf16[256,256]{1,0:T(8,128)(2,1)}, u32[]{:S(2)}) copy-start(bf16[256,256]{1,0:T(8,128)(2,1)} %param.9) | copy-start | bytes 393220
  59.8 1.0 copy-start.1
  60.8 34.5 %reduce-scatter.5.cloned.1.call-start = ((), (), s32[]{:S(2)}) async-start(), calls=%async_computation.5 | async-start | bytes 393216 | tf_op jit(solution)/shard_map/reduce_scatter | solution.py:46
  70.7 0.7 copy-start.4
  88.2 56.1 %copy-start.9 = (s32[1,16]{1,0:T(1,128)S(1)}, s32[1,16]{1,0:T(1,128)}, u32[]{:S(2)}) copy-start(s32[1,16]{1,0:T(1,128)} %param.15) | copy-start | bytes 196
  88.2 56.1 %all-to-all-start.1 = ((f32[16,128,256]{2,1,0:T(8,128)}), f32[16,128,256]{2,1,0:T(8,128)}, u32[]{:S(2)}, u32[]{:S(2)}) async-start(f32[16,128,256]{2,1,0:T(8,128)} %slice.15), calls=%async_computation.2 | async-start | bytes 4194304 | tf_op jit(solution)/shard_map/all_to_all | solution.py:37
  95.3 78.3 %all-gather.3.cloned.1.call-start = ((), (), s32[]{:S(2)}) async-start(), calls=%async_computation.6 | async-start | bytes 2228224 | tf_op jit(solution)/shard_map/all_gather | solution.py:47
  144.3 4.2 %copy-start.5 = (bf16[4,128,256]{2,1,0:T(8,128)(2,1)S(1)}, bf16[4,128,256]{2,1,0:T(8,128)(2,1)}, u32[]{:S(2)}) copy-start(bf16[4,128,256]{2,1,0:T(8,128)(2,1)} %copy-done.4) | copy-start | bytes 786436
Sparse Core Ops, SparseCore 0:
  60.9 8.6 reduce-scatter.2
  72.5 8.9 reduce-scatter.4
  98.8 74.7 all-gather.2
